TPU v7x, 32 devices: a whole 2x2x4 slice. The times are simulated.
32 devices in a mesh: section: 2 (over x), seq: 8 (over z, y), rep: 2 (over core).
Axes of the slice: x: 2, y: 2, z: 4, core: 2. Of those that a mesh axis runs over, the one named last changes fastest.
Arguments:
- queries: bfloat16 [512, 2560], P('seq', ('section', 'rep')), may hold values from -5 to 5
- keys: bfloat16 [512, 2560], P('seq', ('section', 'rep')), may hold values from -5 to 5
- values: bfloat16 [512, 2560], P('seq', ('section', 'rep')), may hold values from -6 to 6
- block_order: int32 [16], replicated, may hold values from 0 to 15, each once
- wo: bfloat16 [2560, 5120], P(('section', 'rep'), 'seq'), may hold values from -0.125 to 0.125
- resid: bfloat16 [4, 5120, 128], P(('section', 'rep'), 'seq'), may hold values from -60 to 60
- gain: bfloat16 [5120], P('seq'), may hold values from 0.099609375 to 1.8984375
- w_gate: bfloat16 [13824, 5120], P('seq'), may hold values from -0.078125 to 0.078125
- w_up: bfloat16 [13824, 5120], P('seq'), may hold values from -0.078125 to 0.078125
- w_down: bfloat16 [13824, 5120], P('seq'), may hold values from -0.0625 to 0.0625
Outputs:
- mixed: bfloat16 [4, 5120, 128], P(('section', 'rep'), 'seq')
Inputs may be any that keep to these rules, and one draw needn't show every extreme that they name: `block_order`: each number once.
All inputs are finite; a program needn't handle non-finite values.
Results may differ from a plain program's by a relative error of at most 0.0055.
Values may be sent and summed in bfloat16 or wider, within the bound.
A program may use at most 128 MiB of HBM per device.

v0:
```python
import jax
import jax.numpy as jnp
from jax import lax
from jax.sharding import PartitionSpec as P

D = 5120
HEAD_DIM = 128


def key_positions(order, start, count, block_rows):
    row_ids = start + jnp.arange(count, dtype=jnp.int32)
    owners = row_ids // block_rows
    match = owners[:, None] == jnp.arange(order.shape[0], dtype=jnp.int32)[None, :]
    first = jnp.sum(jnp.where(match, order[None, :], 0), axis=1)
    return first * block_rows + row_ids % block_rows


def on_device(queries, keys, values, block_order, wo, resid, gain, w_gate, w_up, w_down):
    seq_dev = queries.shape[0]
    heads_dev = queries.shape[1] // HEAD_DIM
    groups = lax.axis_size("section") * lax.axis_size("rep")
    n_seq = lax.axis_size("seq")
    sub_rows = seq_dev // groups
    block_rows = seq_dev // 2
    query_start = lax.axis_index("seq") * seq_dev
    query_pos = key_positions(block_order, query_start, seq_dev, block_rows)
    query_heads = queries.reshape(seq_dev, heads_dev, HEAD_DIM)
    scale = HEAD_DIM ** (-0.5)
    running_max = jnp.full((seq_dev, heads_dev), -1e30, jnp.float32)
    key_piece = lax.all_gather(keys, "seq", axis=0, tiled=True)
    value_piece = lax.all_gather(values, "seq", axis=0, tiled=True)
    count = key_piece.shape[0]
    key_pos = key_positions(block_order, jnp.int32(0), count, block_rows)
    scores = (
        jnp.einsum(
            "qhd,khd->qhk",
            query_heads,
            key_piece.reshape(count, heads_dev, HEAD_DIM),
            preferred_element_type=jnp.float32,
        )
        * scale
    )
    visible = (key_pos[None, :] <= query_pos[:, None])[:, None, :]
    new_max = jnp.maximum(running_max, jnp.max(jnp.where(visible, scores, -1e30), axis=-1))
    probs = jnp.where(visible, jnp.exp(scores - new_max[..., None]), 0.0)
    total = jnp.sum(probs, axis=-1)
    weighted = jnp.einsum(
        "qhk,khd->qhd",
        probs.astype(jnp.bfloat16),
        value_piece.reshape(count, heads_dev, HEAD_DIM),
        preferred_element_type=jnp.float32,
    )
    running_max, total, weighted = (new_max, total, weighted)
    attended = (
        (weighted / total[..., None]).astype(jnp.bfloat16).reshape(seq_dev, heads_dev * HEAD_DIM)
    )
    columns = wo.shape[1]
    token_count = n_seq * sub_rows
    parts = attended.reshape(groups, sub_rows, heads_dev * HEAD_DIM)
    group_rows = lax.all_to_all(parts, ("section", "rep"), split_axis=0, concat_axis=2, tiled=True)
    wo_columns = lax.all_gather(wo, ("section", "rep"), axis=0, tiled=True)
    piece = lax.all_gather(group_rows, "seq", axis=0, tiled=True)
    flat = piece.reshape(piece.shape[0] * piece.shape[1], piece.shape[2])
    product = jnp.dot(flat, wo_columns, preferred_element_type=jnp.float32)
    projected = product.reshape(piece.shape[0], piece.shape[1], columns)
    projected_cols = projected.reshape(token_count, columns).T
    carried = resid.reshape(columns, token_count).astype(jnp.float32) + projected_cols
    squares = lax.psum(jnp.sum(carried * carried, axis=0), "seq")
    normed = (
        carried * lax.rsqrt(squares / D + 1e-05)[None, :] * gain.astype(jnp.float32)[:, None]
    ).astype(jnp.bfloat16)
    piece = lax.all_gather(normed, "seq", axis=0, tiled=True)
    gate_sum = jnp.dot(w_gate, piece, preferred_element_type=jnp.float32)
    up_sum = jnp.dot(w_up, piece, preferred_element_type=jnp.float32)
    hidden = (jax.nn.silu(gate_sum) * up_sum).astype(jnp.bfloat16)
    term = lax.dot_general(
        w_down, hidden, (((0,), (0,)), ((), ())), preferred_element_type=jnp.float32
    )
    down = lax.psum_scatter(term, "seq", scatter_dimension=0, tiled=True)
    return (carried + down).astype(jnp.bfloat16).reshape(resid.shape)


def solution(mesh):
    return jax.shard_map(
        on_device,
        mesh=mesh,
        in_specs=(
            P("seq", ("section", "rep")),
            P("seq", ("section", "rep")),
            P("seq", ("section", "rep")),
            P(),
            P(("section", "rep"), "seq"),
            P(("section", "rep"), "seq", None),
            P("seq"),
            P("seq", None),
            P("seq", None),
            P("seq", None),
        ),
        out_specs=P(("section", "rep"), "seq", None),
        check_vma=False,
    )
```

profile of v0, /device:TPU:0, one launch (start us, length us, event | category | flops | bytes accessed | tf_op | source)
XLA Modules:
  0.0 288.4 jit_solution(9217807981591576571)
XLA Ops:
  6.5 0.0 copy-start
  6.5 0.0 copy-start.5
  6.5 0.0 all-gather.3.cloned.1.call-start
  6.5 0.7 all-gather.3.cloned.1.call-update
  7.3 33.6 %all_gather.15 = bf16[512,640]{1,0:T(8,128)(2,1)S(1)} all-gather(bf16[64,640]{1,0:T(8,128)(2,1)} %param.11), channel_id=1, replica_groups=mesh['section'=2,'seq'=8,'rep'=2] {'seq'}, dimensions={0}, use_global_device_ids=true | all-gather | bytes 737280 | tf_op jit(solution)/shard_map/all_gather | solution.py:30
  40.9 0.3 copy.33
  41.1 0.0 copy-start.3
  41.2 31.9 %all_gather.16 = bf16[512,640]{1,0:T(8,128)(2,1)S(1)} all-gather(bf16[64,640]{1,0:T(8,128)(2,1)} %param.12), channel_id=1, replica_groups=mesh['section'=2,'seq'=8,'rep'=2] {'seq'}, dimensions={0}, use_global_device_ids=true | all-gather | bytes 737280 | tf_op jit(solution)/shard_map/all_gather | solution.py:31
  73.1 0.0 copy-start.4
  73.1 0.3 copy.36
  73.4 0.0 copy-done.5
  73.4 0.1 select_reduce_fusion.2
  73.5 0.1 select_reduce_fusion.1
  73.6 0.1 broadcast_compare_fusion
  73.7 0.0 copy-done
  73.7 0.3 select_reduce_fusion
  74.0 0.3 fusion.6
  74.3 0.4 fusion.5
  74.7 0.1 copy.38
  74.7 0.7 reshape_reshape.3
  75.5 3.3 %all-to-all-start = ((bf16[4,16,640]{2,1,0:T(8,128)(2,1)}), bf16[4,16,640]{2,1,0:T(8,128)(2,1)S(1)}, u32[]{:S(2)}, u32[]{:S(2)}) async-start(bf16[4,16,640]{2,1,0:T(8,128)(2,1)} %reshape_reshape.3), calls=%async_computation | async-start | bytes 163840 | tf_op jit(solution)/shard_map/all_to_all | solution.py:60
  78.8 0.0 all-gather.5.cloned.1.call-start
  78.8 0.0 copy-done.3
  78.9 0.2 copy.32
  79.0 0.0 copy-done.4
  79.0 3.9 %all-to-all-done = bf16[4,16,640]{2,1,0:T(8,128)(2,1)S(1)} async-done(((bf16[4,16,640]{2,1,0:T(8,128)(2,1)}), bf16[4,16,640]{2,1,0:T(8,128)(2,1)S(1)}, u32[]{:S(2)}, u32[]{:S(2)}) %all-to-all-start) | async-done | bytes 81952 | tf_op jit(solution)/shard_map/all_to_all | solution.py:60
  83.0 31.7 %all_gather.17 = bf16[8,16,2560]{2,1,0:T(8,128)(2,1)S(1)} all-gather(bf16[1,16,2560]{2,1,0:T(8,128)(2,1)S(1)} %bitcast.59), channel_id=1, replica_groups=mesh['section'=2,'seq'=8,'rep'=2] {'seq'}, dimensions={0}, use_global_device_ids=true | all-gather | bytes 737280 | tf_op jit(solution)/shard_map/all_gather | solution.py:62
  114.6 0.0 all-gather.3.cloned.1.call-done
  114.6 2.7 multiply_reduce_fusion
  117.3 21.5 %psum.7 = f32[128]{0:T(128)S(1)} all-reduce(f32[128]{0:T(128)S(1)} %get-tuple-element.7), channel_id=1, replica_groups=mesh['section'=2,'seq'=8,'rep'=2] {'seq'}, use_global_device_ids=true, to_apply=%region_5.6 | all-reduce | flops 128 | bytes 1024 | tf_op jit(solution)/shard_map/psum | solution.py:68
  138.9 0.8 multiply_convert_fusion
  139.6 0.0 all-gather.5.cloned.1.call-update
  139.7 0.0 reduce-scatter.2.cloned.1.call-start
  139.7 38.9 %all-gather.5.cloned.1.call-done = bf16[5120,128]{0,1:T(8,128)(2,1)} async-done(((bf16[640,128]{0,1:T(8,128)(2,1)}), bf16[5120,128]{0,1:T(8,128)(2,1)}) %all-gather.5.cloned.1.call-update) | async-done | bytes 1310736 | tf_op jit(solution)/shard_map/all_gather | solution.py:72
  178.6 0.0 copy-start.2
  178.6 11.1 %convolution_bitcast_fusion.2 = f32[1728,128]{1,0:T(8,128)S(1)} fusion(bf16[5120,128]{0,1:T(8,128)(2,1)} %all-gather.5.cloned.1.call-done, bf16[1728,5120]{1,0:T(8,128)(2,1)} %param.17), kind=kOutput, calls=%fused_computation.3 | convolution fusion | flops 2264924160 | bytes 19890176 | tf_op jit(solution)/shard_map/dot_general | solution.py:73
  189.7 0.0 copy-done.2
  189.7 0.0 copy-start.1
  189.7 20.6 %convolution_bitcast_fusion = f32[5120,128]{0,1:T(8,128)} fusion(bf16[1728,5120]{1,0:T(8,128)(2,1)} %param.19, bf16[5120,128]{0,1:T(8,128)(2,1)S(1)} %copy-done.2, bf16[1728,5120]{1,0:T(8,128)(2,1)} %param.18, f32[1728,128]{1,0:T(8,128)S(1)} %convolution_bitcast_fusion.2), kind=kOutput, calls=%fused_computation | convolution fusion | flops 4531175424 | bytes 40206336 | tf_op jit(solution)/shard_map/dot_general | solution.py:76
  210.4 0.0 reduce-scatter.2.cloned.1.call-update
  210.4 69.7 %reduce-scatter.2.cloned.1.call-done = f32[640,128]{0,1:T(8,128)} async-done(((f32[5120,128]{0,1:T(8,128)}), f32[640,128]{0,1:T(8,128)}) %reduce-scatter.2.cloned.1.call-update) | async-done | bytes 327696 | tf_op jit(solution)/shard_map/reduce_scatter | solution.py:79
  280.1 1.0 fusion.13
  281.1 0.8 copy.40
  281.9 0.0 copy-done.1
  (8 shorter events, 0.1 us)
Async XLA Ops:
  6.5 67.1 %copy-start = (bf16[64,640]{1,0:T(8,128)(2,1)S(1)}, bf16[64,640]{1,0:T(8,128)(2,1)}, u32[]{:S(2)}) copy-start(bf16[64,640]{1,0:T(8,128)(2,1)} %param.10) | copy-start | bytes 245764
  6.5 66.8 %copy-start.5 = (s32[16]{0:T(128)S(1)}, s32[16]{0:T(128)}, u32[]{:S(2)}) copy-start(s32[16]{0:T(128)} %param.13) | copy-start | bytes 196
  6.5 108.1 %all-gather.3.cloned.1.call-start = ((), (), s32[]{:S(2)}) async-start(), calls=%async_computation.2 | async-start | bytes 4096000 | tf_op jit(solution)/shard_map/all_gather | solution.py:61
  41.1 37.7 %copy-start.3 = (bf16[1,640,128]{2,1,0:T(8,128)(2,1)S(1)}, bf16[1,640,128]{2,1,0:T(8,128)(2,1)}, u32[]{:S(2)}) copy-start(bf16[1,640,128]{2,1,0:T(8,128)(2,1)} %param.15) | copy-start | bytes 491524
  73.1 5.9 %copy-start.4 = (bf16[640]{0:T(1024)(128)(2,1)S(1)}, bf16[640]{0:T(1024)(128)(2,1)}, u32[]{:S(2)}) copy-start(bf16[640]{0:T(1024)(128)(2,1)} %param.16) | copy-start | bytes 3844
  75.5 7.5 %all-to-all-start = ((bf16[4,16,640]{2,1,0:T(8,128)(2,1)}), bf16[4,16,640]{2,1,0:T(8,128)(2,1)S(1)}, u32[]{:S(2)}, u32[]{:S(2)}) async-start(bf16[4,16,640]{2,1,0:T(8,128)(2,1)} %reshape_reshape.3), calls=%async_computation | async-start | bytes 163840 | tf_op jit(solution)/shard_map/all_to_all | solution.py:60
  78.8 99.8 %all-gather.5.cloned.1.call-start = ((), (), s32[]{:S(2)}) async-start(), calls=%async_computation.3 | async-start | bytes 1474560 | tf_op jit(solution)/shard_map/all_gather | solution.py:72
  139.7 140.4 %reduce-scatter.2.cloned.1.call-start = ((), (), s32[]{:S(2)}) async-start(), calls=%async_computation.4 | async-start | bytes 2949120 | tf_op jit(solution)/shard_map/reduce_scatter | solution.py:79
  178.6 11.1 %copy-start.2 = (bf16[5120,128]{0,1:T(8,128)(2,1)S(1)}, bf16[5120,128]{0,1:T(8,128)(2,1)}, u32[]{:S(2)}) copy-start(bf16[5120,128]{0,1:T(8,128)(2,1)} %all-gather.5.cloned.1.call-done) | copy-start | bytes 3932164
  189.7 92.2 %copy-start.1 = (bf16[64,640]{1,0:T(8,128)(2,1)S(1)}, bf16[64,640]{1,0:T(8,128)(2,1)}, u32[]{:S(2)}) copy-start(bf16[64,640]{1,0:T(8,128)(2,1)} %param.10) | copy-start | bytes 245764
Sparse Core Ops, SparseCore 0:
  8.9 31.9 all-gather.2
  139.8 38.8 all-gather.4
  210.5 69.5 reduce-scatter.1
where the time goes:
time: 289 us; the launch traced here: 288 us
  blocking collectives  119 us (41%)
  waiting for transfers between devices  113 us (39%)
  matrix products  35.1 us (12%)
  between operations  13.3 us (5%)
  starting transfers between devices  3.38 us (1%)
    reduce_scatter x1, waiting for transfers between devices, on_device(): down = lax.psum_scatter(term, 'seq', scatter_dimension=0, tiled=True)  69.7 us
    all_gather x1, waiting for transfers between devices, on_device(): piece = lax.all_gather(normed, 'seq', axis=0, tiled=True)  38.9 us
    all_gather x1, blocking collectives, on_device(): key_piece = lax.all_gather(keys, 'seq', axis=0, tiled=True)  33.6 us
    all_gather x1, blocking collectives, on_device(): value_piece = lax.all_gather(values, 'seq', axis=0, tiled=True)  31.9 us
    all_gather x1, blocking collectives, on_device(): piece = lax.all_gather(group_rows, 'seq', axis=0, tiled=True)  31.7 us
    psum x1, blocking collectives, on_device(): squares = lax.psum(jnp.sum(carried * carried, axis=0), 'seq')  21.5 us
    dot_general x1, matrix products, on_device(): lax.dot_general(w_down, hidden, (((0,), (0,)), ((), ())), preferred_eleme...  20.6 us
    dot_general x1, matrix products, on_device(): gate_sum = jnp.dot(w_gate, piece, preferred_element_type=jnp.float32)  11.1 us
  transfers between devices with their start and end apart: 4, of which 3 were waited for; matrix products, arithmetic and copies ran while one was open for 1% of the time, Pallas kernels for 0%

commit v1 on v0

--- a/solution.py
+++ b/solution.py
@@ -65,7 +65,7 @@
     projected = product.reshape(piece.shape[0], piece.shape[1], columns)
     projected_cols = projected.reshape(token_count, columns).T
     carried = resid.reshape(columns, token_count).astype(jnp.float32) + projected_cols
-    squares = lax.psum(jnp.sum(carried * carried, axis=0), "seq")
+    squares = jnp.sum(lax.all_gather(jnp.sum(carried * carried, axis=0), "seq"), axis=0)
     normed = (
         carried * lax.rsqrt(squares / D + 1e-05)[None, :] * gain.astype(jnp.float32)[:, None]
     ).astype(jnp.bfloat16)

time: 289 us -> 288 us (level)
    psum x1 -> x0, blocking collectives: 21.5 us -> none  [on_device(): squares = lax.psum(jnp.sum(carried * carried, axis=0), 'seq')]
    all_gather x0 -> x1, blocking collectives: none -> 20.7 us  [on_device(): lax.all_gather(jnp.sum(carried * carried, axis=0), 'seq')]
where the time goes in v1:
time: 288 us; the launch traced here: 287 us
  blocking collectives  118 us (41%)
  waiting for transfers between devices  113 us (39%)
  matrix products  35.1 us (12%)
  between operations  13.3 us (5%)
  starting transfers between devices  3.38 us (1%)
    reduce_scatter x1, waiting for transfers between devices, on_device(): down = lax.psum_scatter(term, 'seq', scatter_dimension=0, tiled=True)  69.5 us
    all_gather x1, waiting for transfers between devices, on_device(): piece = lax.all_gather(normed, 'seq', axis=0, tiled=True)  38.9 us
    all_gather x1, blocking collectives, on_device(): key_piece = lax.all_gather(keys, 'seq', axis=0, tiled=True)  33.6 us
    all_gather x1, blocking collectives, on_device(): value_piece = lax.all_gather(values, 'seq', axis=0, tiled=True)  31.9 us
    all_gather x1, blocking collectives, on_device(): piece = lax.all_gather(group_rows, 'seq', axis=0, tiled=True)  31.7 us
    all_gather x1, blocking collectives, on_device(): lax.all_gather(jnp.sum(carried * carried, axis=0), 'seq')  20.7 us
    dot_general x1, matrix products, on_device(): lax.dot_general(w_down, hidden, (((0,), (0,)), ((), ())), preferred_eleme...  20.6 us
    dot_general x1, matrix products, on_device(): gate_sum = jnp.dot(w_gate, piece, preferred_element_type=jnp.float32)  11.1 us
  transfers between devices with their start and end apart: 4, of which 3 were waited for; matrix products, arithmetic and copies ran while one was open for 1% of the time, Pallas kernels for 0%

profile of v1, /device:TPU:0, one launch (start us, length us, event | category | flops | bytes accessed | tf_op | source)
XLA Modules:
  0.0 287.4 jit_solution(7449797971163525646)
XLA Ops:
  6.5 0.0 copy-start
  6.5 0.0 copy-start.5
  6.5 0.0 all-gather.5.cloned.1.call-start
  6.5 0.7 all-gather.5.cloned.1.call-update
  7.3 33.6 %all_gather.21 = bf16[512,640]{1,0:T(8,128)(2,1)S(1)} all-gather(bf16[64,640]{1,0:T(8,128)(2,1)} %param.11), channel_id=1, replica_groups=mesh['section'=2,'seq'=8,'rep'=2] {'seq'}, dimensions={0}, use_global_device_ids=true | all-gather | bytes 737280 | tf_op jit(solution)/shard_map/all_gather | solution.py:30
  40.9 0.3 copy.33
  41.1 0.0 copy-start.3
  41.2 31.9 %all_gather.22 = bf16[512,640]{1,0:T(8,128)(2,1)S(1)} all-gather(bf16[64,640]{1,0:T(8,128)(2,1)} %param.12), channel_id=1, replica_groups=mesh['section'=2,'seq'=8,'rep'=2] {'seq'}, dimensions={0}, use_global_device_ids=true | all-gather | bytes 737280 | tf_op jit(solution)/shard_map/all_gather | solution.py:31
  73.1 0.0 copy-start.4
  73.1 0.3 copy.36
  73.4 0.0 copy-done.5
  73.4 0.1 select_reduce_fusion.2
  73.5 0.1 select_reduce_fusion.1
  73.6 0.1 broadcast_compare_fusion
  73.7 0.0 copy-done
  73.7 0.3 select_reduce_fusion
  74.0 0.3 fusion.6
  74.3 0.4 fusion.5
  74.7 0.1 copy.38
  74.7 0.7 reshape_reshape.3
  75.5 3.3 %all-to-all-start = ((bf16[4,16,640]{2,1,0:T(8,128)(2,1)}), bf16[4,16,640]{2,1,0:T(8,128)(2,1)S(1)}, u32[]{:S(2)}, u32[]{:S(2)}) async-start(bf16[4,16,640]{2,1,0:T(8,128)(2,1)} %reshape_reshape.3), calls=%async_computation | async-start | bytes 163840 | tf_op jit(solution)/shard_map/all_to_all | solution.py:60
  78.8 0.0 all-gather.7.cloned.1.call-start
  78.8 0.0 copy-done.3
  78.9 0.2 copy.32
  79.0 0.0 copy-done.4
  79.0 3.9 %all-to-all-done = bf16[4,16,640]{2,1,0:T(8,128)(2,1)S(1)} async-done(((bf16[4,16,640]{2,1,0:T(8,128)(2,1)}), bf16[4,16,640]{2,1,0:T(8,128)(2,1)S(1)}, u32[]{:S(2)}, u32[]{:S(2)}) %all-to-all-start) | async-done | bytes 81952 | tf_op jit(solution)/shard_map/all_to_all | solution.py:60
  83.0 31.7 %all_gather.23 = bf16[8,16,2560]{2,1,0:T(8,128)(2,1)S(1)} all-gather(bf16[1,16,2560]{2,1,0:T(8,128)(2,1)S(1)} %bitcast.60), channel_id=1, replica_groups=mesh['section'=2,'seq'=8,'rep'=2] {'seq'}, dimensions={0}, use_global_device_ids=true | all-gather | bytes 737280 | tf_op jit(solution)/shard_map/all_gather | solution.py:62
  114.6 0.0 all-gather.5.cloned.1.call-done
  114.6 2.7 multiply_reduce_fusion
  117.3 20.7 %all-gather.1 = f32[8,1,128]{2,1,0:T(1,128)S(1)} all-gather(f32[1,1,128]{2,1,0:T(1,128)S(1)} %bitcast.61), channel_id=2, replica_groups=mesh['section'=2,'seq'=8,'rep'=2] {'seq'}, dimensions={0}, use_global_device_ids=true | all-gather | bytes 4608 | tf_op jit(solution)/shard_map/all_gather | solution.py:68
  138.0 0.8 multiply_convert_fusion
  138.8 0.0 all-gather.7.cloned.1.call-update
  138.8 0.0 reduce-scatter.2.cloned.1.call-start
  138.9 38.9 %all-gather.7.cloned.1.call-done = bf16[5120,128]{0,1:T(8,128)(2,1)} async-done(((bf16[640,128]{0,1:T(8,128)(2,1)}), bf16[5120,128]{0,1:T(8,128)(2,1)}) %all-gather.7.cloned.1.call-update) | async-done | bytes 1310736 | tf_op jit(solution)/shard_map/all_gather | solution.py:72
  177.8 0.0 copy-start.2
  177.8 11.1 %convolution_bitcast_fusion.2 = f32[1728,128]{1,0:T(8,128)S(1)} fusion(bf16[5120,128]{0,1:T(8,128)(2,1)} %all-gather.7.cloned.1.call-done, bf16[1728,5120]{1,0:T(8,128)(2,1)} %param.17), kind=kOutput, calls=%fused_computation.3 | convolution fusion | flops 2264924160 | bytes 19890176 | tf_op jit(solution)/shard_map/dot_general | solution.py:73
  188.9 0.0 copy-done.2
  188.9 0.0 copy-start.1
  188.9 20.6 %convolution_bitcast_fusion = f32[5120,128]{0,1:T(8,128)} fusion(bf16[1728,5120]{1,0:T(8,128)(2,1)} %param.19, bf16[5120,128]{0,1:T(8,128)(2,1)S(1)} %copy-done.2, bf16[1728,5120]{1,0:T(8,128)(2,1)} %param.18, f32[1728,128]{1,0:T(8,128)S(1)} %convolution_bitcast_fusion.2), kind=kOutput, calls=%fused_computation | convolution fusion | flops 4531175424 | bytes 40206336 | tf_op jit(solution)/shard_map/dot_general | solution.py:76
  209.5 0.0 reduce-scatter.2.cloned.1.call-update
  209.5 69.5 %reduce-scatter.2.cloned.1.call-done = f32[640,128]{0,1:T(8,128)} async-done(((f32[5120,128]{0,1:T(8,128)}), f32[640,128]{0,1:T(8,128)}) %reduce-scatter.2.cloned.1.call-update) | async-done | bytes 327696 | tf_op jit(solution)/shard_map/reduce_scatter | solution.py:79
  279.1 1.0 fusion.13
  280.1 0.8 copy.40
  280.9 0.0 copy-done.1
  (9 shorter events, 0.1 us)
Async XLA Ops:
  6.5 67.1 %copy-start = (bf16[64,640]{1,0:T(8,128)(2,1)S(1)}, bf16[64,640]{1,0:T(8,128)(2,1)}, u32[]{:S(2)}) copy-start(bf16[64,640]{1,0:T(8,128)(2,1)} %param.10) | copy-start | bytes 245764
  6.5 66.8 %copy-start.5 = (s32[16]{0:T(128)S(1)}, s32[16]{0:T(128)}, u32[]{:S(2)}) copy-start(s32[16]{0:T(128)} %param.13) | copy-start | bytes 196
  6.5 108.1 %all-gather.5.cloned.1.call-start = ((), (), s32[]{:S(2)}) async-start(), calls=%async_computation.2 | async-start | bytes 4096000 | tf_op jit(solution)/shard_map/all_gather | solution.py:61
  41.1 37.7 %copy-start.3 = (bf16[1,640,128]{2,1,0:T(8,128)(2,1)S(1)}, bf16[1,640,128]{2,1,0:T(8,128)(2,1)}, u32[]{:S(2)}) copy-start(bf16[1,640,128]{2,1,0:T(8,128)(2,1)} %param.15) | copy-start | bytes 491524
  73.1 5.9 %copy-start.4 = (bf16[640]{0:T(1024)(128)(2,1)S(1)}, bf16[640]{0:T(1024)(128)(2,1)}, u32[]{:S(2)}) copy-start(bf16[640]{0:T(1024)(128)(2,1)} %param.16) | copy-start | bytes 3844
  75.5 7.5 %all-to-all-start = ((bf16[4,16,640]{2,1,0:T(8,128)(2,1)}), bf16[4,16,640]{2,1,0:T(8,128)(2,1)S(1)}, u32[]{:S(2)}, u32[]{:S(2)}) async-start(bf16[4,16,640]{2,1,0:T(8,128)(2,1)} %reshape_reshape.3), calls=%async_computation | async-start | bytes 163840 | tf_op jit(solution)/shard_map/all_to_all | solution.py:60
  78.8 99.0 %all-gather.7.cloned.1.call-start = ((), (), s32[]{:S(2)}) async-start(), calls=%async_computation.3 | async-start | bytes 1474560 | tf_op jit(solution)/shard_map/all_gather | solution.py:72
  138.8 140.3 %reduce-scatter.2.cloned.1.call-start = ((), (), s32[]{:S(2)}) async-start(), calls=%async_computation.4 | async-start | bytes 2949120 | tf_op jit(solution)/shard_map/reduce_scatter | solution.py:79
  177.8 11.1 %copy-start.2 = (bf16[5120,128]{0,1:T(8,128)(2,1)S(1)}, bf16[5120,128]{0,1:T(8,128)(2,1)}, u32[]{:S(2)}) copy-start(bf16[5120,128]{0,1:T(8,128)(2,1)} %all-gather.7.cloned.1.call-done) | copy-start | bytes 3932164
  188.9 92.0 %copy-start.1 = (bf16[64,640]{1,0:T(8,128)(2,1)S(1)}, bf16[64,640]{1,0:T(8,128)(2,1)}, u32[]{:S(2)}) copy-start(bf16[64,640]{1,0:T(8,128)(2,1)} %param.10) | copy-start | bytes 245764
Sparse Core Ops, SparseCore 0:
  8.9 31.9 all-gather.4
  138.9 38.8 all-gather.6
  209.7 69.3 reduce-scatter.1
